TPU v7x, 32 devices: a whole 2x2x4 slice. The times are simulated.
32 devices in a mesh: tp: 8 (over z, y), rep: 4 (over x, core).
Axes of the slice: x: 2, y: 2, z: 4, core: 2. Of those that a mesh axis runs over, the one named last changes fastest.
Arguments:
- tokens: bfloat16 [1536, 8192], P('rep', 'tp'), may hold values from -6 to 6
- row_lengths: int32 [8], P('rep'), may hold values from 1 to 192
- attn_gain: float32 [8192], P('tp'), may hold values from 0.1 to 1.9
- query_weight: bfloat16 [8192, 4096], P('rep', 'tp'), may hold values from -2 to 2
- key_weight: bfloat16 [8192, 512], P('rep', 'tp'), may hold values from -2 to 2
- value_matrix: bfloat16 [8192, 512], P('rep', 'tp'), may hold values from -0.0625 to 0.0625
- output_weight: bfloat16 [4096, 8192], P('rep', 'tp'), may hold values from -0.09375 to 0.09375
- final_gain: float32 [8192], P('tp'), may hold values from 0.1 to 1.9
- value_head: float32 [8192, 6], P('tp'), may hold values from -0.0625 to 0.0625
Outputs:
- resid_out: bfloat16 [1536, 8192], P('rep', 'tp')
- objective_scores: float32 [1536, 6], P('rep')
All inputs are finite; a program needn't handle non-finite values.
Results may differ from a plain program's by a relative error of at most 0.025.
Values may be sent and summed in bfloat16 or wider, within the bound.
A program may use at most 64 MiB of HBM per device.

v0:
```python
import jax
import jax.numpy as jnp
from jax import lax
from jax.sharding import PartitionSpec as P

KEY_VALUE_HEADS = 4
HEAD_SIZE = 128
EPS = 1e-05


def local(
    tokens,
    row_lengths,
    attn_gain,
    query_weight,
    key_weight,
    value_matrix,
    output_weight,
    final_gain,
    value_head,
):
    width = tokens.shape[1] * lax.axis_size("tp")
    xfloat = tokens.astype(jnp.float32)
    total = lax.psum(jnp.sum(xfloat * xfloat, axis=1), "tp")
    first_scale = lax.rsqrt(total / width + EPS)[:, None]
    normed = lax.all_gather(
        (xfloat * first_scale * attn_gain).astype(jnp.bfloat16), "tp", axis=1, tiled=True
    )
    rows_here = normed.shape[0]
    head_cols = query_weight.shape[1]
    pieces = (
        lax.all_gather(query_weight, "rep", axis=0, tiled=True),
        lax.all_gather(key_weight, "rep", axis=0, tiled=True),
        lax.all_gather(value_matrix, "rep", axis=0, tiled=True),
    )
    columns = normed
    query, key_rows, value_rows = tuple(
        (jnp.dot(columns, piece, preferred_element_type=jnp.float32) for piece in pieces)
    )
    query = query.astype(jnp.bfloat16)
    key_rows = key_rows.astype(jnp.bfloat16)
    value_rows = value_rows.astype(jnp.bfloat16)
    key_full, value_full = (
        lax.all_gather(key_rows, "tp", axis=1, tiled=True),
        lax.all_gather(value_rows, "tp", axis=1, tiled=True),
    )
    local_heads = head_cols // HEAD_SIZE
    sequence_rows = row_lengths.shape[0]
    row_length_count = rows_here // sequence_rows
    first_head = lax.axis_index("tp") * local_heads
    key_value_index = (first_head + jnp.arange(local_heads, dtype=jnp.int32)) % KEY_VALUE_HEADS
    query4 = query.reshape(sequence_rows, row_length_count, local_heads, HEAD_SIZE)
    key_tensor4 = jnp.take(
        key_full.reshape(sequence_rows, row_length_count, KEY_VALUE_HEADS, HEAD_SIZE),
        key_value_index,
        axis=2,
    )
    value_tensor4 = jnp.take(
        value_full.reshape(sequence_rows, row_length_count, KEY_VALUE_HEADS, HEAD_SIZE),
        key_value_index,
        axis=2,
    )
    scores = jnp.einsum(
        "rqhd,rkhd->rhqk", query4, key_tensor4, preferred_element_type=jnp.float32
    ) * (1.0 / HEAD_SIZE**0.5)
    position = jnp.arange(row_length_count, dtype=jnp.int32)
    causal = position[None, :] <= position[:, None]
    allowed = causal[None, None, :, :] & (
        position[None, None, None, :] < row_lengths[:, None, None, None]
    )
    scores = jnp.where(allowed, scores, jnp.float32(-1e30))
    scores = scores - jnp.max(scores, axis=3, keepdims=True)
    expo = jnp.exp(scores)
    probs = (expo / jnp.sum(expo, axis=3, keepdims=True)).astype(jnp.bfloat16)
    attended = jnp.einsum(
        "rhqk,rkhd->rqhd", probs, value_tensor4, preferred_element_type=jnp.float32
    )
    attended = attended.astype(jnp.bfloat16).reshape(rows_here, head_cols)
    mixed_all = lax.all_gather(attended, "tp", axis=1, tiled=True)
    columns = mixed_all
    update = jnp.dot(
        columns,
        lax.all_gather(output_weight, "rep", axis=0, tiled=True),
        preferred_element_type=jnp.float32,
    )
    resid_out = (xfloat + update).astype(jnp.bfloat16)
    rfloat = resid_out.astype(jnp.float32)
    squares = jnp.sum(rfloat * rfloat, axis=1)
    local_scores = jnp.dot(rfloat * final_gain, value_head, precision=lax.Precision.HIGHEST)
    total_out, weighted = lax.psum((squares, local_scores), "tp")
    logits = weighted * lax.rsqrt(total_out / width + EPS)[:, None]
    live = (position[None, :] < row_lengths[:, None]).reshape(rows_here, 1)
    objective_scores = jnp.where(live, logits, jnp.float32(0.0))
    return (resid_out, objective_scores)


def solution(mesh):
    in_specs = (
        P("rep", "tp"),
        P("rep"),
        P("tp"),
        P("rep", "tp"),
        P("rep", "tp"),
        P("rep", "tp"),
        P("rep", "tp"),
        P("tp"),
        P("tp", None),
    )
    out_specs = (P("rep", "tp"), P("rep", None))
    return jax.shard_map(local, mesh=mesh, in_specs=in_specs, out_specs=out_specs, check_vma=False)
```

profile of v0, /device:TPU:0, one launch (start us, length us, event | category | flops | bytes accessed | tf_op | source)
XLA Modules:
  0.0 382.7 jit_solution(16926781889026036177)
XLA Ops:
  7.2 0.0 copy-start
  7.2 0.0 copy-start.1
  7.2 0.0 all-gather.9.cloned.1.call-start
  7.2 0.7 all-gather.9.cloned.1.call-update
  7.9 0.0 all-gather.7.cloned.1.call-start
  8.0 1.4 fusion.4
  9.3 23.1 %psum.21 = f32[384]{0:T(512)S(1)} all-reduce(f32[384]{0:T(512)S(1)} %fusion.4), channel_id=1, replica_groups=mesh['tp'=8,'rep'=4] {'tp'}, use_global_device_ids=true, to_apply=%region_1.0 | all-reduce | flops 384 | bytes 3072 | tf_op jit(solution)/shard_map/psum | solution.py:24
  32.5 0.0 copy-done.1
  32.5 1.8 fusion.6
  34.3 0.0 all-gather.7.cloned.1.call-update
  34.3 0.0 all-gather.13.cloned.1.call-start
  34.4 0.7 all-gather.13.cloned.1.call-update
  35.1 0.0 all-gather.11.cloned.1.call-start
  35.1 0.5 all-gather.11.cloned.1.call-update
  35.7 0.0 copy-start.4
  35.7 0.0 all-gather.17.cloned.1.call-start
  35.7 0.5 all-gather.17.cloned.1.call-update
  36.3 0.0 all-gather.15.cloned.1.call-start
  36.4 0.0 copy-done.4
  36.4 0.1 iota_compare_fusion.1
  36.5 0.1 broadcast_and_fusion
  36.6 0.0 all-gather.9.cloned.1.call-done
  36.6 93.9 %all-gather.7.cloned.1.call-done = bf16[384,8192]{1,0:T(8,128)(2,1)} async-done(((bf16[384,1024]{1,0:T(8,128)(2,1)}), bf16[384,8192]{1,0:T(8,128)(2,1)}) %all-gather.7.cloned.1.call-update) | async-done | bytes 6291472 | tf_op jit(solution)/shard_map/all_gather | solution.py:26
  130.5 5.1 %convolution_convert_fusion.3 = bf16[384,64]{0,1:T(8,128)(2,1)S(1)} fusion(bf16[384,8192]{1,0:T(8,128)(2,1)} %all-gather.7.cloned.1.call-done, bf16[8192,64]{0,1:T(8,128)(2,1)} %all-gather.9.cloned.1.call-done), kind=kOutput, calls=%fused_computation.22 | convolution fusion | flops 402677760 | bytes 7389184 | tf_op jit(solution)/shard_map/dot_general | solution.py:38
  135.6 31.0 %all_gather.26 = bf16[384,512]{0,1:T(8,128)(2,1)S(1)} all-gather(bf16[384,64]{0,1:T(8,128)(2,1)S(1)} %convolution_convert_fusion.3), channel_id=1, replica_groups=mesh['tp'=8,'rep'=4] {'tp'}, dimensions={1}, use_global_device_ids=true | all-gather | bytes 442368 | tf_op jit(solution)/shard_map/all_gather | solution.py:45
  166.6 0.3 reshape.108
  166.8 0.4 copy.14
  167.3 0.0 all-gather.13.cloned.1.call-done
  167.3 5.1 %convolution_convert_fusion.2 = bf16[384,64]{0,1:T(8,128)(2,1)S(1)} fusion(bf16[384,8192]{1,0:T(8,128)(2,1)} %all-gather.7.cloned.1.call-done, bf16[8192,64]{0,1:T(8,128)(2,1)} %all-gather.13.cloned.1.call-done), kind=kOutput, calls=%fused_computation.21 | convolution fusion | flops 402677760 | bytes 7389184 | tf_op jit(solution)/shard_map/dot_general | solution.py:38
  172.4 31.1 %all_gather.29 = bf16[384,512]{0,1:T(8,128)(2,1)S(1)} all-gather(bf16[384,64]{0,1:T(8,128)(2,1)S(1)} %convolution_convert_fusion.2), channel_id=1, replica_groups=mesh['tp'=8,'rep'=4] {'tp'}, dimensions={1}, use_global_device_ids=true | all-gather | bytes 442368 | tf_op jit(solution)/shard_map/all_gather | solution.py:44
  203.6 0.3 reshape.109
  203.8 0.4 copy.16
  204.3 0.6 gather_fusion
  204.9 0.6 gather_fusion.1
  205.6 0.1 select_bitcast_fusion.1
  205.7 1.0 all-gather.11.cloned.1.call-done
  206.7 8.6 %convolution_convert_fusion.1 = bf16[384,512]{1,0:T(8,128)(2,1)S(1)} fusion(bf16[384,8192]{1,0:T(8,128)(2,1)} %all-gather.7.cloned.1.call-done, bf16[8192,512]{1,0:T(8,128)(2,1)} %all-gather.11.cloned.1.call-done), kind=kOutput, calls=%fused_computation.19 | convolution fusion | flops 3221422080 | bytes 15073280 | tf_op jit(solution)/shard_map/dot_general | solution.py:38
  215.3 0.1 reshape.83
  215.4 1.9 fusion.26
  217.3 2.0 fusion.9
  219.3 0.3 copy.21
  219.6 0.8 copy.47
  220.4 0.0 all-gather.15.cloned.1.call-update
  220.5 0.1 lt.45
  220.5 0.0 copy-start.3
  220.5 45.9 %all-gather.17.cloned.1.call-done = bf16[4096,1024]{1,0:T(8,128)(2,1)} async-done(((bf16[1024,1024]{1,0:T(8,128)(2,1)}), bf16[4096,1024]{1,0:T(8,128)(2,1)}) %all-gather.17.cloned.1.call-update) | async-done | bytes 8388624 | tf_op jit(solution)/shard_map/all_gather | solution.py:83
  266.4 65.2 %all-gather.15.cloned.1.call-done = bf16[384,4096]{1,0:T(8,128)(2,1)} async-done(((bf16[384,512]{1,0:T(8,128)(2,1)}), bf16[384,4096]{1,0:T(8,128)(2,1)}) %all-gather.15.cloned.1.call-update) | async-done | bytes 3145744 | tf_op jit(solution)/shard_map/all_gather | solution.py:79
  331.6 7.9 %fusion.3 = (f32[384]{0:T(512)S(1)}, bf16[384,1024]{1,0:T(8,128)(2,1)S(1)}) fusion(bf16[384,4096]{1,0:T(8,128)(2,1)} %all-gather.15.cloned.1.call-done, bf16[4096,1024]{1,0:T(8,128)(2,1)} %all-gather.17.cloned.1.call-done, bf16[384,1024]{1,0:T(8,128)(2,1)S(1)} %copy-done.1), kind=kOutput, calls=%fused_computation.10 | convolution fusion | flops 3223584256 | bytes 13108736 | tf_op jit(solution)/shard_map/dot_general | solution.py:81
  339.4 0.0 copy-start.2
  339.4 0.0 copy-done
  339.4 0.0 copy-done.3
  339.4 1.5 fusion.2
  340.9 34.3 %all-reduce = (f32[384,6]{0,1:T(8,128)S(1)}, f32[384]{0:T(512)S(1)}) all-reduce(f32[384,6]{0,1:T(8,128)S(1)} %fusion.2, f32[384]{0:T(512)S(1)} %get-tuple-element.9), channel_id=1, replica_groups=mesh['tp'=8,'rep'=4] {'tp'}, use_global_device_ids=true, to_apply=%region_4.6 | all-reduce | flops 2688 | bytes 21504 | tf_op jit(solution)/shard_map/psum | solution.py:90
  375.2 0.6 multiply_select_fusion.1
  375.8 0.0 copy-done.2
  (6 shorter events, 0.1 us)
Async XLA Ops:
  7.2 332.3 %copy-start = (f32[1024,6]{0,1:T(8,128)S(1)}, f32[1024,6]{0,1:T(8,128)}, u32[]{:S(2)}) copy-start(f32[1024,6]{0,1:T(8,128)} %param.19) | copy-start | bytes 73732
  7.2 25.3 %copy-start.1 = (bf16[384,1024]{1,0:T(8,128)(2,1)S(1)}, bf16[384,1024]{1,0:T(8,128)(2,1)}, u32[]{:S(2)}) copy-start(bf16[384,1024]{1,0:T(8,128)(2,1)} %param.11) | copy-start | bytes 2359300
  7.2 29.4 %all-gather.9.cloned.1.call-start = ((), (), s32[]{:S(2)}) async-start(), calls=%async_computation.1 | async-start | bytes 1310720 | tf_op jit(solution)/shard_map/all_gather | solution.py:34
  7.9 122.6 %all-gather.7.cloned.1.call-start = ((), (), s32[]{:S(2)}) async-start(), calls=%async_computation | async-start | bytes 7077888 | tf_op jit(solution)/shard_map/all_gather | solution.py:26
  34.3 133.0 %all-gather.13.cloned.1.call-start = ((), (), s32[]{:S(2)}) async-start(), calls=%async_computation.3 | async-start | bytes 1310720 | tf_op jit(solution)/shard_map/all_gather | solution.py:33
  35.1 171.6 %all-gather.11.cloned.1.call-start = ((), (), s32[]{:S(2)}) async-start(), calls=%async_computation.2 | async-start | bytes 10485760 | tf_op jit(solution)/shard_map/all_gather | solution.py:32
  35.7 0.7 copy-start.4
  35.7 230.7 %all-gather.17.cloned.1.call-start = ((), (), s32[]{:S(2)}) async-start(), calls=%async_computation.5 | async-start | bytes 10485760 | tf_op jit(solution)/shard_map/all_gather | solution.py:83
  36.3 295.3 %all-gather.15.cloned.1.call-start = ((), (), s32[]{:S(2)}) async-start(), calls=%async_computation.4 | async-start | bytes 3538944 | tf_op jit(solution)/shard_map/all_gather | solution.py:79
  220.5 118.9 %copy-start.3 = (f32[1024]{0:T(1024)S(1)}, f32[1024]{0:T(1024)}, u32[]{:S(2)}) copy-start(f32[1024]{0:T(1024)} %param.18) | copy-start | bytes 12292
  339.4 36.4 %copy-start.2 = (bf16[384,1024]{1,0:T(8,128)(2,1)}, bf16[384,1024]{1,0:T(8,128)(2,1)S(1)}, u32[]{:S(2)}) copy-start(bf16[384,1024]{1,0:T(8,128)(2,1)S(1)} %get-tuple-element.10) | copy-start | bytes 2359300
Sparse Core Ops, SparseCore 0:
  9.6 19.4 all-gather.8
  34.5 95.9 all-gather.6
  132.1 14.8 all-gather.12
  148.4 58.2 all-gather.10
  208.1 58.2 all-gather.16
  268.9 62.6 all-gather.14
where the time goes:
time: 383 us
  waiting for transfers between devices  208 us (54%)
  blocking collectives  120 us (31%)
  matrix products  32 us (8%)
  between operations  14.3 us (4%)
  other arithmetic  4.2 us (1%)
  local copies, waits for them, and re-layouts  4.01 us (1%)
    all_gather x1, waiting for transfers between devices, local(): lax.all_gather((xfloat * first_scale * attn_gain).astype(jnp.bfloat16), '...  93.9 us
    all_gather x1, waiting for transfers between devices, local(): mixed_all = lax.all_gather(attended, 'tp', axis=1, tiled=True)  65.2 us
    all_gather x1, waiting for transfers between devices, local(): lax.all_gather(output_weight, 'rep', axis=0, tiled=True)  45.9 us
    psum x1, blocking collectives, local(): total_out, weighted = lax.psum((squares, local_scores), 'tp')  34.3 us
    all_gather x1, blocking collectives, local(): lax.all_gather(key_rows, 'tp', axis=1, tiled=True)  31.1 us
    all_gather x1, blocking collectives, local(): lax.all_gather(value_rows, 'tp', axis=1, tiled=True)  31 us
    psum x1, blocking collectives, local(): total = lax.psum(jnp.sum(xfloat * xfloat, axis=1), 'tp')  23.1 us
    dot_general x3, matrix products, local(): jnp.dot(columns, piece, preferred_element_type=jnp.float32)  18.8 us
  transfers between devices with their start and end apart: 6, of which 4 were waited for; matrix products, arithmetic and copies ran while one was open for 8% of the time, Pallas kernels for 0%

commit v1 on v0

--- a/solution.py
+++ b/solution.py
@@ -6,6 +6,16 @@
 KEY_VALUE_HEADS = 4
 HEAD_SIZE = 128
 EPS = 1e-05
+
+
+def around_the_ring(x, mesh_axis, dim):
+    size = lax.axis_size(mesh_axis)
+    held, blocks = (x, [x])
+    for _ in range(size - 1):
+        held = lax.ppermute(held, mesh_axis, [(i, (i + 1) % size) for i in range(size)])
+        blocks.insert(0, held)
+    line = jnp.concatenate(blocks, axis=dim)
+    return jnp.roll(line, (lax.axis_index(mesh_axis) + 1) * x.shape[dim], axis=dim)
 
 
 def local(
@@ -76,7 +86,7 @@
         "rhqk,rkhd->rqhd", probs, value_tensor4, preferred_element_type=jnp.float32
     )
     attended = attended.astype(jnp.bfloat16).reshape(rows_here, head_cols)
-    mixed_all = lax.all_gather(attended, "tp", axis=1, tiled=True)
+    mixed_all = around_the_ring(attended, "tp", 1)
     columns = mixed_all
     update = jnp.dot(
         columns,

time: 383 us -> 367 us (0.958)
  waiting for transfers between devices: 208 us -> 179 us
  local copies, waits for them, and re-layouts: 4.01 us -> 20.3 us
    ppermute x0 -> x7, waiting for transfers between devices: none -> 81.1 us  [around_the_ring(): lax.ppermute(held, mesh_axis, [(i, (i + 1) % size) for i in range(size)])]
    all_gather x1 -> x0, waiting for transfers between devices: 65.2 us -> none  [local(): mixed_all = lax.all_gather(attended, 'tp', axis=1, tiled=True)]
    all_gather x1, waiting for transfers between devices: 45.9 us -> 0.01 us  [local(): lax.all_gather(output_weight, 'rep', axis=0, tiled=True)]
    unnamed x11 -> x26, local copies, waits for them, and re-layouts: 0.83 us -> 16.4 us
  transfers between devices with their start and end apart: 6 -> 12, of which waited for: 4 -> 9; matrix products, arithmetic and copies ran while one was open for 8% -> 12% of each run, Pallas kernels for 0% -> 0%
where the time goes in v1:
time: 367 us
  waiting for transfers between devices  179 us (49%)
  blocking collectives  118 us (32%)
  matrix products  29.3 us (8%)
  local copies, waits for them, and re-layouts  20.3 us (6%)
  between operations  14 us (4%)
  other arithmetic  4.65 us (1%)
    all_gather x1, waiting for transfers between devices, local(): lax.all_gather((xfloat * first_scale * attn_gain).astype(jnp.bfloat16), '...  93.9 us
    ppermute x7, waiting for transfers between devices, around_the_ring(): lax.ppermute(held, mesh_axis, [(i, (i + 1) % size) for i in range(size)])  81.1 us
    psum x1, blocking collectives, local(): total_out, weighted = lax.psum((squares, local_scores), 'tp')  33 us
    all_gather x1, blocking collectives, local(): lax.all_gather(value_rows, 'tp', axis=1, tiled=True)  31 us
    all_gather x1, blocking collectives, local(): lax.all_gather(key_rows, 'tp', axis=1, tiled=True)  31 us
    psum x1, blocking collectives, local(): total = lax.psum(jnp.sum(xfloat * xfloat, axis=1), 'tp')  23.1 us
    dot_general x3, matrix products, local(): jnp.dot(columns, piece, preferred_element_type=jnp.float32)  18.8 us
    unnamed x26, local copies, waits for them, and re-layouts  16.4 us
  transfers between devices with their start and end apart: 12, of which 9 were waited for; matrix products, arithmetic and copies ran while one was open for 12% of the time, Pallas kernels for 0%

profile of v1, /device:TPU:0, one launch (start us, length us, event | category | flops | bytes accessed | tf_op | source)
XLA Modules:
  0.0 366.8 jit_solution(5129945124729496308)
XLA Ops:
  7.2 0.0 all-gather.8.cloned.1.call-start
  7.2 0.7 all-gather.8.cloned.1.call-update
  7.9 0.0 all-gather.6.cloned.1.call-start
  8.0 1.4 fusion.6
  9.3 23.1 %psum.21 = f32[384]{0:T(512)S(1)} all-reduce(f32[384]{0:T(512)S(1)} %fusion.6), channel_id=1, replica_groups=mesh['tp'=8,'rep'=4] {'tp'}, use_global_device_ids=true, to_apply=%region_1.0 | all-reduce | flops 384 | bytes 3072 | tf_op jit(solution)/shard_map/psum | solution.py:34
  32.5 2.3 fusion.8
  34.8 0.0 all-gather.12.cloned.1.call-start
  34.8 0.7 all-gather.12.cloned.1.call-update
  35.5 0.0 all-gather.10.cloned.1.call-start
  35.6 0.5 all-gather.10.cloned.1.call-update
  36.1 0.0 all-gather.14.cloned.1.call-start
  36.1 0.5 all-gather.14.cloned.1.call-update
  36.8 0.1 iota_compare_fusion.1
  36.9 0.1 broadcast_and_fusion
  37.0 0.0 all-gather.8.cloned.1.call-done
  37.0 93.9 %all-gather.6.cloned.1.call-done = bf16[384,8192]{1,0:T(8,128)(2,1)} async-done(((bf16[384,1024]{1,0:T(8,128)(2,1)}), bf16[384,8192]{1,0:T(8,128)(2,1)}) %all-gather.6.cloned.1.call-update) | async-done | bytes 6291472 | tf_op jit(solution)/shard_map/all_gather | solution.py:36
  130.9 5.1 %convolution_convert_fusion.3 = bf16[384,64]{0,1:T(8,128)(2,1)S(1)} fusion(bf16[384,8192]{1,0:T(8,128)(2,1)} %all-gather.6.cloned.1.call-done, bf16[8192,64]{0,1:T(8,128)(2,1)} %all-gather.8.cloned.1.call-done), kind=kOutput, calls=%fused_computation.24 | convolution fusion | flops 402677760 | bytes 7389184 | tf_op jit(solution)/shard_map/dot_general | solution.py:48
  136.0 31.0 %all_gather.23 = bf16[384,512]{0,1:T(8,128)(2,1)S(1)} all-gather(bf16[384,64]{0,1:T(8,128)(2,1)S(1)} %convolution_convert_fusion.3), channel_id=1, replica_groups=mesh['tp'=8,'rep'=4] {'tp'}, dimensions={1}, use_global_device_ids=true | all-gather | bytes 442368 | tf_op jit(solution)/shard_map/all_gather | solution.py:55
  167.0 0.3 reshape.108
  167.2 0.4 copy.14
  167.7 0.0 all-gather.12.cloned.1.call-done
  167.7 5.1 %convolution_convert_fusion.2 = bf16[384,64]{0,1:T(8,128)(2,1)S(1)} fusion(bf16[384,8192]{1,0:T(8,128)(2,1)} %all-gather.6.cloned.1.call-done, bf16[8192,64]{0,1:T(8,128)(2,1)} %all-gather.12.cloned.1.call-done), kind=kOutput, calls=%fused_computation.23 | convolution fusion | flops 402677760 | bytes 7389184 | tf_op jit(solution)/shard_map/dot_general | solution.py:48
  172.8 31.0 %all_gather.26 = bf16[384,512]{0,1:T(8,128)(2,1)S(1)} all-gather(bf16[384,64]{0,1:T(8,128)(2,1)S(1)} %convolution_convert_fusion.2), channel_id=1, replica_groups=mesh['tp'=8,'rep'=4] {'tp'}, dimensions={1}, use_global_device_ids=true | all-gather | bytes 442368 | tf_op jit(solution)/shard_map/all_gather | solution.py:54
  203.8 0.3 reshape.109
  204.1 0.4 copy.16
  204.5 0.6 gather_fusion
  205.1 0.6 gather_fusion.1
  205.8 0.1 select_bitcast_fusion.1
  205.9 1.2 all-gather.10.cloned.1.call-done
  207.1 8.6 %convolution_convert_fusion.1 = bf16[384,512]{1,0:T(8,128)(2,1)S(1)} fusion(bf16[384,8192]{1,0:T(8,128)(2,1)} %all-gather.6.cloned.1.call-done, bf16[8192,512]{1,0:T(8,128)(2,1)} %all-gather.10.cloned.1.call-done), kind=kOutput, calls=%fused_computation.21 | convolution fusion | flops 3221422080 | bytes 15073280 | tf_op jit(solution)/shard_map/dot_general | solution.py:48
  215.7 0.1 reshape.83
  215.8 0.7 fusion.31
  216.5 0.5 fusion.13
  217.0 0.3 copy.21
  217.3 0.1 copy.51
  217.4 1.5 collective-permute-start
  218.9 12.5 %collective-permute-done = bf16[384,512]{1,0:T(8,128)(2,1)S(1)} collective-permute-done((bf16[384,512]{1,0:T(8,128)(2,1)S(1)}, bf16[384,512]{1,0:T(8,128)(2,1)S(1)}, u32[]{:S(2)}, u32[]{:S(2)}) %collective-permute-start) | collective-permute-done | bytes 393248 | tf_op jit(solution)/shard_map/ppermute | solution.py:15
  231.4 13.1 %collective-permute-done.1 = bf16[384,512]{1,0:T(8,128)(2,1)S(1)} collective-permute-done((bf16[384,512]{1,0:T(8,128)(2,1)S(1)}, bf16[384,512]{1,0:T(8,128)(2,1)S(1)}, u32[]{:S(2)}, u32[]{:S(2)}) %collective-permute-start.1) | collective-permute-done | bytes 393248 | tf_op jit(solution)/shard_map/ppermute | solution.py:15
  244.5 12.3 %collective-permute-done.2 = bf16[384,512]{1,0:T(8,128)(2,1)S(1)} collective-permute-done((bf16[384,512]{1,0:T(8,128)(2,1)S(1)}, bf16[384,512]{1,0:T(8,128)(2,1)S(1)}, u32[]{:S(2)}, u32[]{:S(2)}) %collective-permute-start.2) | collective-permute-done | bytes 393248 | tf_op jit(solution)/shard_map/ppermute | solution.py:15
  256.8 11.4 %collective-permute-done.3 = bf16[384,512]{1,0:T(8,128)(2,1)S(1)} collective-permute-done((bf16[384,512]{1,0:T(8,128)(2,1)S(1)}, bf16[384,512]{1,0:T(8,128)(2,1)S(1)}, u32[]{:S(2)}, u32[]{:S(2)}) %collective-permute-start.3) | collective-permute-done | bytes 393248 | tf_op jit(solution)/shard_map/ppermute | solution.py:15
  268.2 10.5 %collective-permute-done.4 = bf16[384,512]{1,0:T(8,128)(2,1)S(1)} collective-permute-done((bf16[384,512]{1,0:T(8,128)(2,1)S(1)}, bf16[384,512]{1,0:T(8,128)(2,1)S(1)}, u32[]{:S(2)}, u32[]{:S(2)}) %collective-permute-start.4) | collective-permute-done | bytes 393248 | tf_op jit(solution)/shard_map/ppermute | solution.py:15
  278.7 10.6 %collective-permute-done.5 = bf16[384,512]{1,0:T(8,128)(2,1)} collective-permute-done((bf16[384,512]{1,0:T(8,128)(2,1)S(1)}, bf16[384,512]{1,0:T(8,128)(2,1)}, u32[]{:S(2)}, u32[]{:S(2)}) %collective-permute-start.5) | collective-permute-done | bytes 393248 | tf_op jit(solution)/shard_map/ppermute | solution.py:15
  289.3 0.1 lt.59
  289.4 10.7 %collective-permute-done.6 = bf16[384,512]{1,0:T(8,128)(2,1)} collective-permute-done((bf16[384,512]{1,0:T(8,128)(2,1)}, bf16[384,512]{1,0:T(8,128)(2,1)}, u32[]{:S(2)}, u32[]{:S(2)}) %collective-permute-start.6) | collective-permute-done | bytes 393248 | tf_op jit(solution)/shard_map/ppermute | solution.py:15
  300.1 1.8 constant_dynamic-update-slice_fusion.15
  301.9 1.8 constant_dynamic-update-slice_fusion.14
  303.7 0.8 constant_dynamic-update-slice_fusion.13
  304.5 0.8 constant_dynamic-update-slice_fusion.12
  305.3 0.9 constant_dynamic-update-slice_fusion.11
  306.1 0.9 constant_dynamic-update-slice_fusion.10
  307.0 0.9 constant_dynamic-update-slice_fusion.9
  307.9 0.9 constant_dynamic-update-slice_fusion.8
  308.7 1.8 constant_dynamic-update-slice_fusion.7
  310.5 1.8 constant_dynamic-update-slice_fusion.6
  312.4 0.8 constant_dynamic-update-slice_fusion.5
  313.2 0.8 constant_dynamic-update-slice_fusion.4
  314.0 0.8 constant_dynamic-update-slice_fusion.3
  314.8 0.8 constant_dynamic-update-slice_fusion.2
  315.6 0.8 constant_dynamic-update-slice_fusion.1
  316.4 0.8 constant_dynamic-update-slice_fusion
  317.2 7.9 %fusion.5 = (f32[384]{0:T(512)S(1)}, bf16[384,1024]{1,0:T(8,128)(2,1)S(1)}) fusion(bf16[4096,1024]{1,0:T(8,128)(2,1)} %all-gather.14.cloned.1.call-done, bf16[384,8192]{1,0:T(8,128)(2,1)} %constant_dynamic-update-slice_fusion, s32[]{:T(128)S(6)} %select_n.37, bf16[384,1024]{1,0:T(8,128)(2,1)S(1)} %copy-done.1), kind=kOutput, calls=%fused_computation.12 | convolution fusion | flops 3223584256 | bytes 13108740 | tf_op jit(solution)/shard_map/dot_general | solution.py:91
  325.1 1.5 fusion.4
  326.6 33.0 %all-reduce = (f32[384,6]{0,1:T(8,128)S(1)}, f32[384]{0:T(512)S(1)}) all-reduce(f32[384,6]{0,1:T(8,128)S(1)} %fusion.4, f32[384]{0:T(512)S(1)} %get-tuple-element.9), channel_id=1, replica_groups=mesh['tp'=8,'rep'=4] {'tp'}, use_global_device_ids=true, to_apply=%region_4.6 | all-reduce | flops 2688 | bytes 21504 | tf_op jit(solution)/shard_map/psum | solution.py:100
  359.6 0.6 multiply_select_fusion.1
  (24 shorter events, 0.1 us)
Async XLA Ops:
  7.2 317.9 %copy-start = (f32[1024,6]{0,1:T(8,128)S(1)}, f32[1024,6]{0,1:T(8,128)}, u32[]{:S(2)}) copy-start(f32[1024,6]{0,1:T(8,128)} %param.19) | copy-start | bytes 73732
  7.2 29.6 %copy-start.4 = (s32[2]{0:T(128)S(1)}, s32[2]{0:T(128)}, u32[]{:S(2)}) copy-start(s32[2]{0:T(128)} %param.12) | copy-start | bytes 28
  7.2 29.8 %all-gather.8.cloned.1.call-start = ((), (), s32[]{:S(2)}) async-start(), calls=%async_computation.1 | async-start | bytes 1310720 | tf_op jit(solution)/shard_map/all_gather | solution.py:44
  7.9 123.0 %all-gather.6.cloned.1.call-start = ((), (), s32[]{:S(2)}) async-start(), calls=%async_computation | async-start | bytes 7077888 | tf_op jit(solution)/shard_map/all_gather | solution.py:36
  34.8 132.9 %all-gather.12.cloned.1.call-start = ((), (), s32[]{:S(2)}) async-start(), calls=%async_computation.3 | async-start | bytes 1310720 | tf_op jit(solution)/shard_map/all_gather | solution.py:43
  35.5 171.6 %all-gather.10.cloned.1.call-start = ((), (), s32[]{:S(2)}) async-start(), calls=%async_computation.2 | async-start | bytes 10485760 | tf_op jit(solution)/shard_map/all_gather | solution.py:42
  36.1 281.1 %all-gather.14.cloned.1.call-start = ((), (), s32[]{:S(2)}) async-start(), calls=%async_computation.4 | async-start | bytes 10485760 | tf_op jit(solution)/shard_map/all_gather | solution.py:93
  217.4 14.0 %collective-permute-start = (bf16[384,512]{1,0:T(8,128)(2,1)S(1)}, bf16[384,512]{1,0:T(8,128)(2,1)S(1)}, u32[]{:S(2)}, u32[]{:S(2)}) collective-permute-start(bf16[384,512]{1,0:T(8,128)(2,1)S(1)} %bitcast.30), channel_id=1, source_target_pairs={{0,4},{4,8},{8,12},{12,16},{16,20},{20,24},{24,28},{28,0},{1,5},{5... | collective-permute-start | bytes 1179656 | tf_op jit(solution)/shard_map/ppermute | solution.py:15
  231.4 13.1 %collective-permute-start.1 = (bf16[384,512]{1,0:T(8,128)(2,1)S(1)}, bf16[384,512]{1,0:T(8,128)(2,1)S(1)}, u32[]{:S(2)}, u32[]{:S(2)}) collective-permute-start(bf16[384,512]{1,0:T(8,128)(2,1)S(1)} %collective-permute-done), channel_id=1, source_target_pairs={{0,4},{4,8},{8,12},{12,16},{16,20},{20,24},{24,28},{28,0},{1,5},{5... | collective-permute-start | bytes 1179656 | tf_op jit(solution)/shard_map/ppermute | solution.py:15
  244.5 12.3 %collective-permute-start.2 = (bf16[384,512]{1,0:T(8,128)(2,1)S(1)}, bf16[384,512]{1,0:T(8,128)(2,1)S(1)}, u32[]{:S(2)}, u32[]{:S(2)}) collective-permute-start(bf16[384,512]{1,0:T(8,128)(2,1)S(1)} %collective-permute-done.1), channel_id=1, source_target_pairs={{0,4},{4,8},{8,12},{12,16},{16,20},{20,24},{24,28},{28,0},{1,5},{5... | collective-permute-start | bytes 1179656 | tf_op jit(solution)/shard_map/ppermute | solution.py:15
  256.8 11.4 %collective-permute-start.3 = (bf16[384,512]{1,0:T(8,128)(2,1)S(1)}, bf16[384,512]{1,0:T(8,128)(2,1)S(1)}, u32[]{:S(2)}, u32[]{:S(2)}) collective-permute-start(bf16[384,512]{1,0:T(8,128)(2,1)S(1)} %collective-permute-done.2), channel_id=1, source_target_pairs={{0,4},{4,8},{8,12},{12,16},{16,20},{20,24},{24,28},{28,0},{1,5},{5... | collective-permute-start | bytes 1179656 | tf_op jit(solution)/shard_map/ppermute | solution.py:15
  268.2 10.5 %collective-permute-start.4 = (bf16[384,512]{1,0:T(8,128)(2,1)S(1)}, bf16[384,512]{1,0:T(8,128)(2,1)S(1)}, u32[]{:S(2)}, u32[]{:S(2)}) collective-permute-start(bf16[384,512]{1,0:T(8,128)(2,1)S(1)} %collective-permute-done.3), channel_id=1, source_target_pairs={{0,4},{4,8},{8,12},{12,16},{16,20},{20,24},{24,28},{28,0},{1,5},{5... | collective-permute-start | bytes 1179656 | tf_op jit(solution)/shard_map/ppermute | solution.py:15
  278.7 10.6 %collective-permute-start.5 = (bf16[384,512]{1,0:T(8,128)(2,1)S(1)}, bf16[384,512]{1,0:T(8,128)(2,1)}, u32[]{:S(2)}, u32[]{:S(2)}) collective-permute-start(bf16[384,512]{1,0:T(8,128)(2,1)S(1)} %collective-permute-done.4), channel_id=1, source_target_pairs={{0,4},{4,8},{8,12},{12,16},{16,20},{20,24},{24,28},{28,0},{1,5},{5... | collective-permute-start | bytes 1179656 | tf_op jit(solution)/shard_map/ppermute | solution.py:15
  289.3 10.8 %collective-permute-start.6 = (bf16[384,512]{1,0:T(8,128)(2,1)}, bf16[384,512]{1,0:T(8,128)(2,1)}, u32[]{:S(2)}, u32[]{:S(2)}) collective-permute-start(bf16[384,512]{1,0:T(8,128)(2,1)} %collective-permute-done.5), channel_id=1, source_target_pairs={{0,4},{4,8},{8,12},{12,16},{16,20},{20,24},{24,28},{28,0},{1,5},{5... | collective-permute-start | bytes 1179656 | tf_op jit(solution)/shard_map/ppermute | solution.py:15
  289.4 27.8 %copy-start.1 = (bf16[384,1024]{1,0:T(8,128)(2,1)S(1)}, bf16[384,1024]{1,0:T(8,128)(2,1)}, u32[]{:S(2)}) copy-start(bf16[384,1024]{1,0:T(8,128)(2,1)} %param.11) | copy-start | bytes 2359300
  317.2 7.9 %copy-start.3 = (f32[1024]{0:T(1024)S(1)}, f32[1024]{0:T(1024)}, u32[]{:S(2)}) copy-start(f32[1024]{0:T(1024)} %param.18) | copy-start | bytes 12292
  325.1 35.2 %copy-start.2 = (bf16[384,1024]{1,0:T(8,128)(2,1)}, bf16[384,1024]{1,0:T(8,128)(2,1)S(1)}, u32[]{:S(2)}) copy-start(bf16[384,1024]{1,0:T(8,128)(2,1)S(1)} %get-tuple-element.10) | copy-start | bytes 2359300
Sparse Core Ops, SparseCore 0:
  9.6 19.4 all-gather.7
  34.9 95.9 all-gather.5
  132.5 14.8 all-gather.11
  148.8 58.2 all-gather.9
  208.5 58.2 all-gather.13
